TPU v7x, 128 devices: a whole 4x4x4 slice. The times are simulated.
128 devices in a mesh: rep: 4 (over x), tile: 32 (over z, y, core).
Axes of the slice: x: 4, y: 4, z: 4, core: 2. Of those that a mesh axis runs over, the one named last changes fastest.
Arguments:
- feature_tiles: bfloat16 [256, 16, 128, 128], P(('rep', 'tile')), parts along dimension 0, may hold values from -6 to 6
- neighbours: int32 [256, 4], P('rep'), parts along dimension 0, may hold values from -1 to 63, as said below
- valid_rows: int32 [256], P('rep'), parts along dimension 0, may hold values from 4 to 16, as said below
- tile_image: int32 [256], P('rep'), parts along dimension 0, may hold values from 0 to 31, as said below
- gain_one: float32 [128], replicated, may hold values from 0.1 to 1.9
- shift_one: float32 [128], replicated, may hold values from -3 to 3
- kernel_one: bfloat16 [3, 3, 128, 128], replicated, may hold values from -0.1875 to 0.1875
- offset_one: float32 [128], replicated, may hold values from -3 to 3
- gain_two: float32 [128], replicated, may hold values from 0.1 to 1.9
- shift_two: float32 [128], replicated, may hold values from -3 to 3
- kernel_two: bfloat16 [3, 3, 128, 128], replicated, may hold values from -0.1875 to 0.1875
- offset_two: float32 [128], replicated, may hold values from -3 to 3
Outputs:
- block_out: bfloat16 [256, 16, 128, 128], P(('rep', 'tile')), parts along dimension 0
There are 4 independent parts, one for each index of `rep`. A program takes and returns all parts, laid end to end along the dimension named above; an argument that names none is the same for every part. Nothing has to cross between parts.
Inputs may be any that keep to these rules, and one draw needn't show every extreme that they name: Each image is a rectangle of tiles; neighbours name the adjacent tile of the same image in that direction, or -1 at the image's border. `valid_rows`: only tiles in the bottom row of tiles of an image have fewer than 16 rows; all tiles of that row have the same count. `tile_image`: image numbers need not be consecutive; some may be unused.
All inputs are finite; a program needn't handle non-finite values.
Results may differ from a plain program's by a relative error of at most 0.0075.
Values may be sent and summed in bfloat16 or wider, within the bound.
A program may use at most 64 MiB of HBM per device.

v0:
```python
import jax
import jax.numpy as jnp
from jax import lax
from jax.sharding import PartitionSpec as P

G = 32


epsilon = 1e-06


def in_one_piece(arrays, axis, dim, along):
    both = jnp.concatenate(arrays, axis=along)
    whole, at, outs = (lax.all_gather(both, axis, axis=dim, tiled=True), 0, [])
    for a in arrays:
        outs.append(lax.slice_in_dim(whole, at, at + a.shape[along], axis=along))
        at += a.shape[along]
    return tuple(outs)


def sent_to_all(shard, axis):
    copies = jnp.broadcast_to(shard, (lax.axis_size(axis), *shard.shape))
    return lax.all_to_all(copies, axis, split_axis=0, concat_axis=0, tiled=True)


def taken_together(shard, axis):
    everything = sent_to_all(shard, axis)
    return jnp.sum(everything, axis=0)


def packed_total(arrays, axis):
    ends = [0]
    for a in arrays:
        ends.append(ends[-1] + a.size)
    running = taken_together(jnp.concatenate([a.ravel() for a in arrays]), axis)
    return tuple((running[b:e].reshape(a.shape) for a, b, e in zip(arrays, ends, ends[1:])))


def pick(source, indices):
    clamped = jnp.maximum(indices, 0)
    fetched = jnp.take(source, clamped, axis=0)
    present = (indices >= 0).reshape(indices.shape + (1,) * (fetched.ndim - 1))
    return jnp.where(present, fetched, jnp.zeros_like(fetched))


def across(vertical, neighbours, column):
    return jnp.where(vertical >= 0, neighbours[jnp.maximum(vertical, 0), column], -1)


def widen(feature, own_links, neighbours):
    side_cols = jnp.stack([feature[:, :, 0, :], feature[:, :, -1, :]], axis=1)
    edge_rows = jnp.stack([feature[:, 0], feature[:, -1]], axis=1)
    all_sides, all_rows = in_one_piece((side_cols, edge_rows), "tile", 0, 2)
    left_col = pick(all_sides[:, 1], own_links[:, 2])
    right_col = pick(all_sides[:, 0], own_links[:, 3])
    widened = jnp.concatenate([left_col[:, :, None], feature, right_col[:, :, None]], axis=2)
    upper_slot = own_links[:, 0]
    lower_slot = own_links[:, 1]
    upper_row = jnp.concatenate(
        [
            pick(all_rows[:, 1, -1], across(upper_slot, neighbours, 2))[:, None],
            pick(all_rows[:, 1], upper_slot),
            pick(all_rows[:, 1, 0], across(upper_slot, neighbours, 3))[:, None],
        ],
        axis=1,
    )
    lower_row = jnp.concatenate(
        [
            pick(all_rows[:, 0, -1], across(lower_slot, neighbours, 2))[:, None],
            pick(all_rows[:, 0], lower_slot),
            pick(all_rows[:, 0, 0], across(lower_slot, neighbours, 3))[:, None],
        ],
        axis=1,
    )
    return jnp.concatenate([upper_row[:, None], widened, lower_row[:, None]], axis=1)


def convolve(padded, kernel, offset):
    tile_count, rows_pad, cols_pad, channels = padded.shape
    tile_rows, tile_cols = (rows_pad - 2, cols_pad - 2)
    summed = jnp.zeros((tile_count * tile_rows * tile_cols, kernel.shape[3]), jnp.float32)
    for row_off in range(3):
        for col_off in range(3):
            window = padded[
                :, row_off : row_off + tile_rows, col_off : col_off + tile_cols, :
            ].reshape(-1, channels)
            summed = summed + jnp.dot(
                window, kernel[row_off, col_off], preferred_element_type=jnp.float32
            )
    return summed.reshape(tile_count, tile_rows, tile_cols, -1) + offset


def group_sums(per_tile, member):
    images = jnp.dot(member.T, per_tile)
    return images.reshape(images.shape[0], G, -1).sum(axis=2)


def to_tiles(per_group, member, group_width):
    per_channel = jnp.repeat(per_group, group_width, axis=1)
    return jnp.dot(member, per_channel)


def normalize(feature, row_mask, member, counts, gain_vec, shift_vec):
    group_width = feature.shape[3] // G
    mask_full = row_mask[:, :, None, None]
    masked = feature * mask_full
    summed_x, squares = packed_total(
        (
            group_sums(jnp.sum(masked, axis=(1, 2)), member),
            group_sums(jnp.sum(masked * feature, axis=(1, 2)), member),
        ),
        "tile",
    )
    means = summed_x / counts
    variance = squares / counts - means * means
    centred = (feature - to_tiles(means, member, group_width)[:, None, None, :]) * mask_full
    inverse = lax.rsqrt(to_tiles(variance, member, group_width) + epsilon)
    normed = centred * inverse[:, None, None, :] * gain_vec + shift_vec
    return (jax.nn.silu(normed) * mask_full).astype(jnp.bfloat16)


def shards(
    feature_tiles,
    neighbours,
    valid_rows,
    tile_image,
    gain_one,
    shift_one,
    kernel_one,
    offset_one,
    gain_two,
    shift_two,
    kernel_two,
    offset_two,
):
    local_count, tile_rows, tile_cols, channels = feature_tiles.shape
    image_count = neighbours.shape[0] // 2
    first_slot = lax.axis_index("tile") * local_count
    own_links = lax.dynamic_slice_in_dim(neighbours, first_slot, local_count, 0)
    own_rows = lax.dynamic_slice_in_dim(valid_rows, first_slot, local_count, 0)
    member_all = (tile_image[:, None] == jnp.arange(image_count)[None, :]).astype(jnp.float32)
    member = lax.dynamic_slice_in_dim(member_all, first_slot, local_count, 0)
    pixels = (valid_rows * tile_cols).astype(jnp.float32)
    counts = jnp.maximum(jnp.dot(member_all.T, pixels[:, None]) * (channels // G), 1.0)
    row_mask = (jnp.arange(tile_rows)[None, :] < own_rows[:, None]).astype(jnp.float32)
    mask_full = row_mask[:, :, None, None]
    inputs = feature_tiles.astype(jnp.float32) * mask_full
    first_act = normalize(inputs, row_mask, member, counts, gain_one, shift_one)
    hidden = (
        convolve(widen(first_act, own_links, neighbours), kernel_one, offset_one) * mask_full
    ).astype(jnp.bfloat16)
    second_act = normalize(
        hidden.astype(jnp.float32), row_mask, member, counts, gain_two, shift_two
    )
    mixed_out = convolve(widen(second_act, own_links, neighbours), kernel_two, offset_two)
    return ((inputs + mixed_out) * mask_full).astype(jnp.bfloat16)


def solution(mesh):
    in_specs = (
        P(("rep", "tile"), None, None, None),
        P("rep", None),
        P("rep"),
        P("rep"),
        P(),
        P(),
        P(),
        P(),
        P(),
        P(),
        P(),
        P(),
    )
    out_specs = P(("rep", "tile"), None, None, None)
    return jax.shard_map(shards, mesh=mesh, in_specs=in_specs, out_specs=out_specs, check_vma=False)
```

profile of v0, /device:TPU:1, one launch (start us, length us, event | category | flops | bytes accessed | tf_op | source)
XLA Modules:
  0.0 192.4 jit_solution(18407619456518038161)
XLA Ops:
  6.5 0.8 dynamic_slice.9
  8.2 1.7 multiply_reduce_fusion
  10.9 0.8 broadcast_in_dim.216
  11.8 9.6 %all-to-all-start = ((f32[32,1,2048]{2,1,0:T(1,128)}), f32[32,1,2048]{2,1,0:T(1,128)S(1)}, u32[]{:S(2)}, u32[]{:S(2)}) async-start(f32[32,1,2048]{2,1,0:T(1,128)} %broadcast_in_dim.216), calls=%async_computation | async-start | bytes 524288 | tf_op jit(solution)/shard_map/all_to_all | solution.py:23
  21.4 0.9 fusion.13
  22.3 8.0 %all-to-all-done = f32[32,1,2048]{2,1,0:T(1,128)S(1)} async-done(((f32[32,1,2048]{2,1,0:T(1,128)}), f32[32,1,2048]{2,1,0:T(1,128)S(1)}, u32[]{:S(2)}, u32[]{:S(2)}) %all-to-all-start) | async-done | bytes 262176 | tf_op jit(solution)/shard_map/all_to_all | solution.py:23
  31.2 1.1 multiply_convert_fusion.5
  35.8 41.9 %all-gather.3.cloned.1.call-done = bf16[64,2,144,128]{3,2,1,0:T(8,128)(2,1)} async-done(((bf16[2,2,144,128]{3,2,1,0:T(8,128)(2,1)}), bf16[64,2,144,128]{3,2,1,0:T(8,128)(2,1)}) %all-gather.3.cloned.1.call-update) | async-done | bytes 4718608 | tf_op jit(solution)/shard_map/all_gather | solution.py:14
  77.7 1.2 fusion.74
  81.6 1.1 slice_bitcast_fusion.7
  84.0 4.1 %slice_bitcast_fusion.2 = (bf16[64,128,128]{2,1,0:T(8,128)(2,1)}, bf16[64,128,128]{2,1,0:T(8,128)(2,1)S(1)}) fusion(bf16[64,2,144,128]{3,2,1,0:T(8,128)(2,1)} %all-gather.3.cloned.1.call-done), kind=kLoop, calls=%fused_computation.50 | loop fusion | bytes 8388608 | tf_op jit(solution)/shard_map/squeeze | solution.py:70
  88.0 2.2 %gather_fusion.10 = bf16[2,128,128]{2,1,0:T(8,128)(2,1)S(1)} fusion(bf16[64,128,128]{2,1,0:T(8,128)(2,1)} %get-tuple-element.40, s32[1024]{0:T(1024)S(1)} %get-tuple-element.111), kind=kCustom, calls=%fused_computation.10.clone | custom fusion | bytes 131080 | tf_op jit(solution)/shard_map/jit(_take)/gather | solution.py:41
  99.4 14.0 %all_to_all.12 = f32[32,1,2048]{2,1,0:T(1,128)S(1)} all-to-all(f32[32,1,2048]{2,1,0:T(1,128)S(1)} %broadcast_in_dim.238), channel_id=1, replica_groups=mesh['rep'=4,'tile'=32] {'tile'}, dimensions={0} | all-to-all | bytes 524288 | tf_op jit(solution)/shard_map/all_to_all | solution.py:23
  114.3 1.0 multiply_convert_fusion.3
  116.2 1.9 %multiply_convert_fusion.1 = bf16[4096,128]{1,0:T(8,128)(2,1)} fusion(f32[4096,128]{1,0:T(8,128)S(1)} %get-tuple-element.106, f32[128]{0:T(128)S(1)} %copy-done.8, f32[128]{0:T(128)S(1)} %copy-done.9, f32[4096]{0:T(1024)S(1)} %bitcast.351, f32[128]{0:T(128)S(1)} %copy-done.7, f32[2,128]{1,0:T(2,128)S(1)} %fusion.10, f32[2,128]{1,0:T(2,128)S(1)} %fusion.86), kind=kLoop, calls=%fused_computation.58 | loop fusion | flops 7864320 | bytes 3165696 | tf_op jit(solution)/shard_map/convert_element_type | solution.py:119
  118.1 42.7 %all-gather.5.cloned.1.call-done = bf16[64,2,144,128]{3,2,1,0:T(8,128)(2,1)} async-done(((bf16[2,2,144,128]{3,2,1,0:T(8,128)(2,1)}), bf16[64,2,144,128]{3,2,1,0:T(8,128)(2,1)}) %all-gather.5.cloned.1.call-update) | async-done | bytes 4718608 | tf_op jit(solution)/shard_map/all_gather | solution.py:14
  160.8 1.2 fusion.73
  164.7 4.1 %slice_bitcast_fusion = (bf16[64,128,128]{2,1,0:T(8,128)(2,1)}, bf16[64,128,128]{2,1,0:T(8,128)(2,1)S(1)}) fusion(bf16[64,2,144,128]{3,2,1,0:T(8,128)(2,1)} %all-gather.5.cloned.1.call-done), kind=kLoop, calls=%fused_computation.48 | loop fusion | bytes 8388608 | tf_op jit(solution)/shard_map/squeeze | solution.py:70
  168.7 2.2 %gather_fusion.18 = bf16[2,128,128]{2,1,0:T(8,128)(2,1)S(1)} fusion(bf16[64,128,128]{2,1,0:T(8,128)(2,1)} %get-tuple-element.32, s32[1024]{0:T(1024)S(1)} %get-tuple-element.111), kind=kCustom, calls=%fused_computation.12.clone | custom fusion | bytes 131080 | tf_op jit(solution)/shard_map/jit(_take)/gather | solution.py:41
  170.9 1.8 slice_bitcast_fusion.5
  172.7 1.5 gather_fusion.15
  180.4 0.8 copy-done.4
  183.3 0.8 copy-done.3
  184.1 1.5 multiply_convert_fusion
  (173 shorter events, 31.7 us)
Async XLA Ops:
  6.5 26.5 %copy-start = (s32[64,4]{0,1:T(4,128)S(1)}, s32[64,4]{0,1:T(4,128)}, u32[]{:S(2)}) copy-start(s32[64,4]{0,1:T(4,128)} %param.19) | copy-start | bytes 3076
  6.5 24.6 %copy-start.2 = (bf16[2,16,128,128]{3,2,1,0:T(8,128)(2,1)S(1)}, bf16[2,16,128,128]{3,2,1,0:T(8,128)(2,1)}, u32[]{:S(2)}) copy-start(bf16[2,16,128,128]{3,2,1,0:T(8,128)(2,1)} %param.18) | copy-start | bytes 3145732
  6.5 24.6 %copy-start.11 = (f32[128]{0:T(128)S(1)}, f32[128]{0:T(128)}, u32[]{:S(2)}) copy-start(f32[128]{0:T(128)} %param.23) | copy-start | bytes 1540
  6.5 24.6 %copy-start.12 = (f32[128]{0:T(128)S(1)}, f32[128]{0:T(128)}, u32[]{:S(2)}) copy-start(f32[128]{0:T(128)} %param.22) | copy-start | bytes 1540
  11.8 18.5 %all-to-all-start = ((f32[32,1,2048]{2,1,0:T(1,128)}), f32[32,1,2048]{2,1,0:T(1,128)S(1)}, u32[]{:S(2)}, u32[]{:S(2)}) async-start(f32[32,1,2048]{2,1,0:T(1,128)} %broadcast_in_dim.216), calls=%async_computation | async-start | bytes 524288 | tf_op jit(solution)/shard_map/all_to_all | solution.py:23
  21.4 56.4 %all-gather.3.cloned.1.call-start = ((), (), s32[]{:S(2)}) async-start(), calls=%async_computation.2 | async-start | bytes 4866048 | tf_op jit(solution)/shard_map/all_gather | solution.py:14
  33.0 127.8 %all-gather.5.cloned.1.call-start = ((), (), s32[]{:S(2)}) async-start(), calls=%async_computation.3 | async-start | bytes 4866048 | tf_op jit(solution)/shard_map/all_gather | solution.py:14
  93.0 1.0 copy-start.5
  96.9 0.7 copy-start.7
  97.6 16.7 %copy-start.8 = (f32[128]{0:T(128)S(1)}, f32[128]{0:T(128)}, u32[]{:S(2)}) copy-start(f32[128]{0:T(128)} %param.27) | copy-start | bytes 1540
  97.6 16.7 %copy-start.9 = (f32[128]{0:T(128)S(1)}, f32[128]{0:T(128)}, u32[]{:S(2)}) copy-start(f32[128]{0:T(128)} %param.26) | copy-start | bytes 1540
  177.7 1.0 copy-start.6
  180.0 1.2 copy-start.4
  182.9 1.2 copy-start.3
  182.9 1.2 copy-start.10
  183.3 2.2 %copy-start.1 = (s32[64,4]{0,1:T(4,128)S(1)}, s32[64,4]{0,1:T(4,128)}, u32[]{:S(2)}) copy-start(s32[64,4]{0,1:T(4,128)} %param.19) | copy-start | bytes 3076
Sparse Core Ops, SparseCore 0:
  33.1 44.5 all-gather.2
  116.3 44.5 all-gather.4
where the time goes:
time: 193 us; the launch traced here: 192 us
  waiting for transfers between devices  92.6 us (48%)
  local copies, waits for them, and re-layouts  38.4 us (20%)
  blocking collectives  14 us (7%)
  between operations  14 us (7%)
  other arithmetic  13.8 us (7%)
  matrix products  10 us (5%)
  starting transfers between devices  9.67 us (5%)
    all_gather x2, waiting for transfers between devices, in_one_piece(): whole, at, outs = (lax.all_gather(both, axis, axis=dim, tiled=True), 0, [])  84.6 us
    all_to_all x1, blocking collectives, sent_to_all(): return lax.all_to_all(copies, axis, split_axis=0, concat_axis=0, tiled=True)  14 us
    gather x16, local copies, waits for them, and re-layouts, pick(): fetched = jnp.take(source, clamped, axis=0)  13.1 us
    all_to_all x1, starting transfers between devices, sent_to_all(): return lax.all_to_all(copies, axis, split_axis=0, concat_axis=0, tiled=True)  9.59 us
    squeeze x2, local copies, waits for them, and re-layouts, widen(): all_rows[:, 0]  8.11 us
    all_to_all x1, waiting for transfers between devices, sent_to_all(): return lax.all_to_all(copies, axis, split_axis=0, concat_axis=0, tiled=True)  7.96 us
    dot_general x18, matrix products, convolve(): jnp.dot(window, kernel[row_off, col_off], preferred_element_type=jnp.floa...  7.78 us
    convert_element_type x3, other arithmetic, normalize(): return (jax.nn.silu(normed) * mask_full).astype(jnp.bfloat16)  4.05 us
  transfers between devices with their start and end apart: 3, of which 3 were waited for; matrix products, arithmetic and copies ran while one was open for 3% of the time, Pallas kernels for 0%

commit v1 on v0

v1 whole, which is shorter than its diff:
```python
import functools

import jax
import jax.numpy as jnp
from jax import lax
from jax.experimental import pallas as pl
from jax.experimental.pallas import tpu as pltpu
from jax.sharding import PartitionSpec as P


N = 32
TILES = 64
TH = 16
TW = 128
C = 128
RING = 144
GROUP = 4
EPS = 1e-06
f32 = jnp.float32
bf16 = jnp.bfloat16


def group_total(v):
    lane = lax.broadcasted_iota(jnp.int32, v.shape, 1)
    t = v + jnp.where(lane % 2 == 0, pltpu.roll(v, C - 1, 1), pltpu.roll(v, 1, 1))
    return t + jnp.where(lane % 4 < 2, pltpu.roll(t, C - 2, 1), pltpu.roll(t, 2, 1))


def kernel(
    x_hbm, nb, vr, ti, gain1, shift1, k1, off1, gain2, shift2, k2, off2,
    out,
    xe, p1, p2, cst, c1, c2s, c2, hc, sa, sb, hid, w1, w2, ec,
    st_send, st, wgt, cnt,
    x_sem, w_sem, p1_send, p1_recv, p2_send, p2_recv, c1_send, c1_recv, c2_send, c2_recv, st_ssem, st_rsem,
):
    me = lax.axis_index("tile")

    barrier = pltpu.get_barrier_semaphore()

    def greet(o, _):
        pl.semaphore_signal(barrier, inc=1, device_id={"tile": lax.rem(me + o, N)}, device_id_type=pl.DeviceIdType.MESH)
        return 0

    lax.fori_loop(1, N, greet, 0)

    x_copy = pltpu.make_async_copy(x_hbm, xe.at[:, 2 : 2 + TH], x_sem)
    x_copy.start()
    w_copies = []
    for conv, (k_hbm, w) in enumerate(((k1, w1), (k2, w2))):
        for half in range(2):
            for e in range(2):
                for o in range(2):
                    a = 2 * half + e - o
                    if 0 <= a <= 2:
                        w_copies.append(
                            pltpu.make_async_copy(
                                k_hbm.at[a],
                                w.at[half, pl.ds(384 * e, 384), pl.ds(128 * o, 128)],
                                w_sem.at[len(w_copies)],
                            )
                        )
    for copy in w_copies:
        copy.start()
    for w in (w1, w2):
        w[0, 0:384, 128:256] = jnp.zeros((384, 128), bf16)
        w[1, 384:768, 0:128] = jnp.zeros((384, 128), bf16)
    hc[...] = jnp.zeros(hc.shape, f32)

    x_copy.wait()

    for t in range(2):
        for side in range(2):
            block = xe[t, 2 : 2 + TH, 112 * side : 112 * side + 16, :].astype(f32)
            ec[side] = block.reshape(TH * 16, C)
        for c in range(4):
            side, at = ((1, 14), (1, 15), (0, 0), (0, 1))[c]
            for h in range(2):
                cst[2 * c + h, t] = ec[side, pl.ds(at + 128 * h, 8, stride=16), :].astype(bf16)

    pl.semaphore_wait(barrier, N - 1)

    def source_row(q):
        return jnp.where(q < 2, 16 + q, q)

    def to_picker(o, _):
        d = lax.rem(me + o, N)
        pltpu.make_async_remote_copy(
            src_ref=xe.at[:, source_row(d // 8), pl.ds(pl.multiple_of(16 * lax.rem(d, 8), 16), 16), :],
            dst_ref=p1.at[pl.ds(2 * me, 2)],
            send_sem=p1_send,
            recv_sem=p1_recv,
            device_id={"tile": d},
            device_id_type=pl.DeviceIdType.MESH,
        ).start()
        return 0

    lax.fori_loop(1, N, to_picker, 0)
    for n in range(8):

        @pl.when(me != 4 * n)
        def _():
            pltpu.make_async_remote_copy(
                src_ref=cst.at[n],
                dst_ref=c1.at[pl.ds(2 * me, 2)],
                send_sem=c1_send,
                recv_sem=c1_recv,
                device_id={"tile": 4 * n},
                device_id_type=pl.DeviceIdType.MESH,
            ).start()

    my_q = me // 8
    my_k = pl.multiple_of(16 * lax.rem(me, 8), 16)
    for t in range(2):
        p1[2 * me + t] = xe[t, source_row(my_q), pl.ds(my_k, 16), :]

    @pl.when(lax.rem(me, 4) == 0)
    def _():
        for t in range(2):
            c1[2 * me + t] = cst[me // 4, t]

    rows = [vr[2 * me + t] for t in range(2)]
    image = [ti[2 * me + t] for t in range(2)]
    links = [[nb[2 * me + t, j] for j in range(4)] for t in range(2)]
    has = [[jnp.where(links[t][j] >= 0, 1.0, 0.0).astype(f32) for j in range(4)] for t in range(2)]

    def own_mask(t, r):
        return jnp.where(r < rows[t], 1.0, 0.0).astype(f32)

    def ring_mask(t, r):
        inside = own_mask(t, r)
        return jnp.where(r < 0, has[t][0], jnp.where(r >= TH, has[t][1], inside))

    lane = lax.broadcasted_iota(jnp.int32, (1, C), 1)
    low = (lane % 4) < 2
    even = (lane % 2) == 0

    def weigh(j, _):
        for t in range(2):
            wa = jnp.where(ti[2 * j] == image[t], 1.0, 0.0).astype(f32)
            wb = jnp.where(ti[2 * j + 1] == image[t], 1.0, 0.0).astype(f32)
            wgt[t, pl.ds(j, 1), :] = jnp.where(low, wa, wb)
        na = (vr[2 * j] * (TW * GROUP)).astype(f32)
        nb_ = (vr[2 * j + 1] * (TW * GROUP)).astype(f32)
        cnt[pl.ds(j, 1), :] = jnp.where(low, na, nb_)
        return 0

    lax.fori_loop(0, N, weigh, 0)

    def statistics(which, row, mask):
        def first(r, accs):
            return tuple(
                accs[t] + jnp.sum(row(t, r).reshape(16, 8, C), axis=0) * mask(t, r) for t in range(2)
            )

        zero = jnp.zeros((8, C), f32)
        sums = lax.fori_loop(0, TH, first, (zero, zero), unroll=2)
        both = jnp.concatenate([jnp.sum(s, axis=0, keepdims=True) for s in sums] + [jnp.zeros((6, C), f32)], axis=0)
        total = group_total(both)
        means = [total[t : t + 1] / (rows[t] * (TW * GROUP)).astype(f32) for t in range(2)]

        def second(r, accs):
            outs = []
            for t in range(2):
                d = row(t, r) - means[t]
                outs.append(accs[t] + jnp.sum((d * d).reshape(16, 8, C), axis=0) * mask(t, r))
            return tuple(outs)

        squares = lax.fori_loop(0, TH, second, (zero, zero), unroll=2)
        both2 = jnp.concatenate([jnp.sum(s, axis=0, keepdims=True) for s in squares] + [jnp.zeros((6, C), f32)], axis=0)
        total2 = group_total(both2)
        packed = jnp.where(
            low,
            jnp.where(even, total[0:1], total2[0:1]),
            jnp.where(even, total[1:2], total2[1:2]),
        )
        st_send[which] = packed
        st[which, me] = packed

        def tell(o, _):
            pltpu.make_async_remote_copy(
                src_ref=st_send.at[which],
                dst_ref=st.at[which, me],
                send_sem=st_ssem.at[which],
                recv_sem=st_rsem.at[which],
                device_id={"tile": lax.rem(me + o, N)},
                device_id_type=pl.DeviceIdType.MESH,
            ).start()
            return 0

        lax.fori_loop(1, N, tell, 0)

    def scales(which, gain, shift):
        got = st.at[which, pl.ds(0, N - 1)]
        pltpu.make_async_copy(got, got, st_rsem.at[which]).wait()
        all_rows = st[which].reshape(N, C)
        counts = cnt[...]
        mean_of = all_rows / counts
        result = []
        for t in range(2):
            w = wgt[t]
            s = jnp.sum(jnp.where(even, w * all_rows, 0.0), axis=0, keepdims=True)
            n = jnp.sum(jnp.where(even, w * counts, 0.0), axis=0, keepdims=True)
            sn = group_total(jnp.concatenate([s, n, jnp.zeros((6, C), f32)], axis=0))
            mean, number = sn[0:1] / sn[1:2], sn[1:2]
            d = mean_of - mean
            m2 = jnp.sum(w * jnp.where(even, counts * d * d, all_rows), axis=0, keepdims=True)
            var = group_total(jnp.concatenate([m2, jnp.zeros((7, C), f32)], axis=0))[0:1] / number
            a = lax.rsqrt(var + EPS) * gain[...]
            result.append((0.5 * a, 0.5 * (shift[...] - mean * a)))
        return result

    statistics(0, lambda t, r: xe[t, 2 + r].astype(f32), own_mask)

    got = p1.at[pl.ds(0, 2 * (N - 1))]
    pltpu.make_async_copy(got, got, p1_recv).wait()
    column = my_q // 2
    ring_row = jnp.where(my_q < 2, my_q, 16 + my_q)

    def to_owner(o, _):
        d = lax.rem(me + o, N)
        for t in range(2):
            p2[d, t] = p1[jnp.maximum(nb[2 * d + t, column], 0)]
        pltpu.make_async_remote_copy(
            src_ref=p2.at[d],
            dst_ref=xe.at[:, ring_row, pl.ds(my_k, 16), :],
            send_sem=p2_send,
            recv_sem=p2_recv,
            device_id={"tile": d},
            device_id_type=pl.DeviceIdType.MESH,
        ).start()
        return 0

    lax.fori_loop(1, N, to_owner, 0)
    for t in range(2):
        xe[t, ring_row, pl.ds(my_k, 16), :] = p1[jnp.maximum(links_of(nb, 2 * me + t, column), 0)]

    @pl.when(lax.rem(me, 4) == 0)
    def _():
        n = me // 4
        got = c1.at[pl.ds(0, 2 * (N - 1))]
        pltpu.make_async_copy(got, got, c1_recv).wait()
        side = jnp.where(n < 4, 2, 3)
        across = jnp.where(lax.rem(n, 2) == 0, 1, 0)

        def pick(d, t, j):
            if j == 0:
                return c1[jnp.maximum(nb[2 * d + t, side], 0)]
            other = jnp.maximum(nb[2 * d + t, across], 0)
            return c1[jnp.maximum(nb[other, side], 0)]

        def column_to_owner(o, _):
            d = lax.rem(me + o, N)
            for t in range(2):
                for j in range(2):
                    c2s[d, t, j] = pick(d, t, j)
            pltpu.make_async_remote_copy(
                src_ref=c2s.at[d],
                dst_ref=c2.at[n],
                send_sem=c2_send,
                recv_sem=c2_recv,
                device_id={"tile": d},
                device_id_type=pl.DeviceIdType.MESH,
            ).start()
            return 0

        lax.fori_loop(1, N, column_to_owner, 0)
        for t in range(2):
            for j in range(2):
                c2[n, t, j] = pick(me, t, j)
        got = c2.at[pl.ds(0, 7)]
        pltpu.make_async_copy(got, got, c2_recv).wait()

    @pl.when(lax.rem(me, 4) != 0)
    def _():
        pltpu.make_async_copy(c2, c2, c2_recv).wait()

    scale1 = scales(0, gain1, shift1)
    got = p1.at[pl.ds(0, 2 * (N - 1))]
    pltpu.make_async_copy(got, got, p2_recv).wait()

    for t in range(2):
        for c in range(4):
            at = (14, 15, 0, 1)[c]
            for h in range(2):
                hc[t, pl.ds(16 * (2 + 8 * h) + at, 8, stride=16), :] = c2[2 * c + h, t, 0].astype(f32)
            hc[t, pl.ds(at, 2, stride=16), :] = c2[2 * c + 1, t, 1].astype(f32)[6:8]
            hc[t, pl.ds(16 * 18 + at, 2, stride=16), :] = c2[2 * c, t, 1].astype(f32)[0:2]

    place = lax.broadcasted_iota(jnp.int32, (16, 1), 0)
    sides = [jnp.where(place < 8, has[t][3], has[t][2]) for t in range(2)]

    def activate(v, a, b):
        u = v * a + b
        return u * jnp.tanh(u) + u

    def norm1(p, _):
        for t in range(2):
            a, b = scale1[t]
            for e in range(2):
                i = 2 * p + e
                m = ring_mask(t, i - 2)
                am, bm = a * m, b * m
                mid = activate(xe[t, i].astype(f32), am, bm)
                end = activate(hc[t, pl.ds(pl.multiple_of(16 * i, 16), 16), :], am * sides[t], bm * sides[t])
                full = jnp.concatenate([mid, end], axis=0)
                before = pltpu.roll(full, 1, 0)
                after = pltpu.roll(full, RING - 1, 0)
                for s, v in enumerate((before, full, after)):
                    sa[t, p, :, pl.ds(384 * e + 128 * s, 128)] = v.astype(bf16)
        return 0

    lax.fori_loop(0, 10, norm1, 0)
    for copy in w_copies[:6]:
        copy.wait()

    bias1 = jnp.concatenate([off1[...], off1[...]], axis=1)
    bias2 = jnp.concatenate([off2[...], off2[...]], axis=1)

    def conv1(step, _):
        t, p0 = step // 3, 3 * lax.rem(step, 3)
        acc = jnp.dot(sa[t, pl.ds(p0, 3)].reshape(3 * RING, 768), w1[0], preferred_element_type=f32)
        acc += jnp.dot(sa[t, pl.ds(p0 + 1, 3)].reshape(3 * RING, 768), w1[1], preferred_element_type=f32)
        h = (acc + bias1).astype(bf16).reshape(3, RING, 256)
        for pp in range(3):
            for e in range(2):
                hid[t, 2 * (p0 + pp) + e] = h[pp, :, 128 * e : 128 * e + 128]
        return 0

    lax.fori_loop(0, 6, conv1, 0)

    statistics(1, lambda t, r: hid[t, 1 + r, 0:TW, :].astype(f32), own_mask)
    for copy in w_copies[6:]:
        copy.wait()
    scale2 = scales(1, gain2, shift2)

    def norm2(p, _):
        for t in range(2):
            a, b = scale2[t]
            for e in range(2):
                i = 2 * p + e
                m = ring_mask(t, i - 1)
                am, bm = a * m, b * m
                h = hid[t, i].astype(f32)
                mid = activate(h[0:TW], am, bm)
                end = activate(h[TW:RING], am * sides[t], bm * sides[t])
                full = jnp.concatenate([mid, end], axis=0)
                before = pltpu.roll(full, 1, 0)
                after = pltpu.roll(full, RING - 1, 0)
                for s, v in enumerate((before, full, after)):
                    sb[t, p, :, pl.ds(384 * e + 128 * s, 128)] = v[0:TW].astype(bf16)
        return 0

    lax.fori_loop(0, 9, norm2, 0)

    def conv2(step, _):
        t, p0 = step // 2, 4 * lax.rem(step, 2)
        acc = jnp.dot(sb[t, pl.ds(p0, 4)].reshape(4 * TW, 768), w2[0], preferred_element_type=f32)
        acc += jnp.dot(sb[t, pl.ds(p0 + 1, 4)].reshape(4 * TW, 768), w2[1], preferred_element_type=f32)
        y = (acc + bias2).reshape(4, TW, 256)
        for pp in range(4):
            for e in range(2):
                r = 2 * (p0 + pp) + e
                v = y[pp, :, 128 * e : 128 * e + 128] + xe[t, 2 + r].astype(f32)
                m = jnp.where(r < jnp.where(t == 0, rows[0], rows[1]), 1.0, 0.0).astype(f32)
                out[t, r] = (v * m).astype(bf16)
        return 0

    lax.fori_loop(0, 4, conv2, 0)

    got = p1.at[pl.ds(0, 2 * (N - 1))]
    pltpu.make_async_copy(got, got, p1_send).wait()
    pltpu.make_async_copy(got, got, p2_send).wait()
    for which in range(2):
        got = st.at[which, pl.ds(0, N - 1)]
        pltpu.make_async_copy(got, got, st_ssem.at[which]).wait()

    @pl.when(lax.rem(me, 4) == 0)
    def _():
        got = cst.at[pl.ds(0, 7)]
        pltpu.make_async_copy(got, got, c1_send).wait()
        got = c2s.at[pl.ds(0, N - 1)]
        pltpu.make_async_copy(got, got, c2_send).wait()

    @pl.when(lax.rem(me, 4) != 0)
    def _():
        pltpu.make_async_copy(cst, cst, c1_send).wait()


def links_of(nb, tile, column):
    return nb[tile, column]


def shards(x, nb, vr, ti, gain1, shift1, kernel1, off1, gain2, shift2, kernel2, off2):
    vmem = pl.BlockSpec(memory_space=pltpu.VMEM)
    smem = pl.BlockSpec(memory_space=pltpu.SMEM)
    anywhere = pl.BlockSpec(memory_space=pl.ANY)
    dma = pltpu.SemaphoreType.DMA
    row = lambda v: v.reshape(1, C)
    return pl.pallas_call(
        kernel,
        out_shape=jax.ShapeDtypeStruct(x.shape, x.dtype),
        in_specs=[anywhere, smem, smem, smem, vmem, vmem, anywhere, vmem, vmem, vmem, anywhere, vmem],
        out_specs=vmem,
        scratch_shapes=[
            pltpu.VMEM((2, TH + 4, TW, C), bf16),
            pltpu.VMEM((TILES, 16, C), bf16),
            pltpu.VMEM((N, 2, 16, C), bf16),
            pltpu.VMEM((8, 2, 8, C), bf16),
            pltpu.VMEM((TILES, 8, C), bf16),
            pltpu.VMEM((N, 2, 2, 8, C), bf16),
            pltpu.VMEM((8, 2, 2, 8, C), bf16),
            pltpu.VMEM((2, 20 * 16, C), f32),
            pltpu.VMEM((2, 10, RING, 768), bf16),
            pltpu.VMEM((2, 9, TW, 768), bf16),
            pltpu.VMEM((2, 18, RING, C), bf16),
            pltpu.VMEM((2, 768, 256), bf16),
            pltpu.VMEM((2, 768, 256), bf16),
            pltpu.VMEM((2, TH * 16, C), f32),
            pltpu.VMEM((2, 1, C), f32),
            pltpu.VMEM((2, N, 1, C), f32),
            pltpu.VMEM((2, N, C), f32),
            pltpu.VMEM((N, C), f32),
            dma,
            dma((12,)),
            dma,
            dma,
            dma,
            dma,
            dma,
            dma,
            dma,
            dma,
            dma((2,)),
            dma((2,)),
        ],
        compiler_params=pltpu.CompilerParams(
            collective_id=0, has_side_effects=True, vmem_limit_bytes=48 * 1024 * 1024
        ),
    )(
        x, nb, vr, ti, row(gain1), row(shift1), kernel1.reshape(3, 3 * C, C), row(off1),
        row(gain2), row(shift2), kernel2.reshape(3, 3 * C, C), row(off2),
    )


def solution(mesh):
    in_specs = (P(("rep", "tile"), None, None, None), P("rep", None), P("rep"), P("rep")) + (P(),) * 8
    out_specs = P(("rep", "tile"), None, None, None)
    return jax.shard_map(shards, mesh=mesh, in_specs=in_specs, out_specs=out_specs, check_vma=False)
```

time: 193 us -> 42.6 us (0.22)
  waiting for transfers between devices: 92.6 us -> 0 us
  Pallas kernels: 0 us -> 36.7 us
  local copies, waits for them, and re-layouts: 38.4 us -> 5.53 us
  blocking collectives: 14 us -> 0 us
  between operations: 14 us -> 0.05 us
  other arithmetic: 13.8 us -> 0 us
  matrix products: 10 us -> 0 us
  starting transfers between devices: 9.67 us -> 0 us
    all_gather x2 -> x0, waiting for transfers between devices: 84.6 us -> none  [in_one_piece(): whole, at, outs = (lax.all_gather(both, axis, axis=dim, tiled=True), 0, [])]
    pallas_call x0 -> x1, Pallas kernels: none -> 36.7 us  [shards(): pl.pallas_call(kernel, out_shape=jax.ShapeDtypeStruct(x.shape, x.dtype),...]
    gather x20 -> x0, local copies, waits for them, and re-layouts: 15.7 us -> none  [the longest x16 13.1 us: pick(): fetched = jnp.take(source, clamped, axis=0)]
    all_to_all x1 -> x0, blocking collectives: 14 us -> none  [sent_to_all(): return lax.all_to_all(copies, axis, split_axis=0, concat_axis=0, tiled=True)]
    squeeze x4 -> x0, local copies, waits for them, and re-layouts: 11 us -> none  [the longest x2 8.11 us: widen(): all_rows[:, 0]]
    dot_general x27 -> x0, matrix products: 10 us -> none  [the longest x18 7.78 us: convolve(): jnp.dot(window, kernel[row_off, col_off], preferred_element_type=jnp.floa...]
    all_to_all x1 -> x0, starting transfers between devices: 9.59 us -> none  [sent_to_all(): return lax.all_to_all(copies, axis, split_axis=0, concat_axis=0, tiled=True)]
    all_to_all x1 -> x0, waiting for transfers between devices: 7.96 us -> none  [sent_to_all(): return lax.all_to_all(copies, axis, split_axis=0, concat_axis=0, tiled=True)]
  transfers between devices with their start and end apart: 3 -> 0, of which waited for: 3 -> 0; matrix products, arithmetic and copies ran while one was open for 3% -> 0% of each run, Pallas kernels for 0% -> 0%
where the time goes in v1:
time: 42.6 us; the launch traced here: 42.3 us
  Pallas kernels  36.7 us (86%)
  local copies, waits for them, and re-layouts  5.53 us (13%)
    pallas_call x1, Pallas kernels, shards(): pl.pallas_call(kernel, out_shape=jax.ShapeDtypeStruct(x.shape, x.dtype),...  36.7 us
    unnamed x26, local copies, waits for them, and re-layouts  5.53 us

profile of v1, /device:TPU:1, one launch (start us, length us, event | category | flops | bytes accessed | tf_op | source)
XLA Modules:
  0.0 42.3 jit_solution(10935511610307529102)
XLA Ops:
  0.0 0.0 copy-start.11
  0.0 0.7 %copy-done.11 = s32[64,4]{0,1:T(4,128)S(1)} copy-done((s32[64,4]{0,1:T(4,128)S(1)}, s32[64,4]{0,1:T(4,128)}, u32[]{:S(2)}) %copy-start.11) | copy-done | bytes 1048
  0.7 0.0 copy-start.3
  0.7 0.0 copy-start.4
  0.7 0.0 copy-start.5
  0.7 0.0 copy-start.6
  0.7 0.0 copy-start.7
  0.7 0.0 copy-start.8
  0.7 0.0 copy-start.9
  0.7 0.0 copy-start.10
  0.7 0.1 copy.13.nb
  0.8 0.5 %copy-done.3 = s32[64]{0:T(128)S(1)} copy-done((s32[64]{0:T(128)S(1)}, s32[64]{0:T(128)}, u32[]{:S(2)}) %copy-start.3) | copy-done | bytes 280
  1.3 0.0 copy-done.4
  1.4 0.0 copy-done.5
  1.4 0.0 copy-done.6
  1.4 0.0 copy-done.7
  1.4 0.0 copy-done.8
  1.4 0.0 copy-done.9
  1.4 0.0 copy-done.10
  1.5 1.2 %copy-done = bf16[2,16,128,128]{3,2,1,0:T(8,128)(2,1)S(1)} copy-done((bf16[2,16,128,128]{3,2,1,0:T(8,128)(2,1)S(1)}, bf16[2,16,128,128]{3,2,1,0:T(8,128)(2,1)}, u32[]{:S(2)}) %copy-start) | copy-done | bytes 1048600
  2.7 1.0 %copy-done.1 = bf16[3,3,128,128]{3,2,1,0:T(8,128)(2,1)S(1)} copy-done((bf16[3,3,128,128]{3,2,1,0:T(8,128)(2,1)S(1)}, bf16[3,3,128,128]{3,2,1,0:T(8,128)(2,1)}, u32[]{:S(2)}) %copy-start.1) | copy-done | bytes 294936
  3.6 1.0 %copy-done.2 = bf16[3,3,128,128]{3,2,1,0:T(8,128)(2,1)S(1)} copy-done((bf16[3,3,128,128]{3,2,1,0:T(8,128)(2,1)S(1)}, bf16[3,3,128,128]{3,2,1,0:T(8,128)(2,1)}, u32[]{:S(2)}) %copy-start.2) | copy-done | bytes 294936
  4.6 36.7 %shard_map.118 = bf16[2,16,128,128]{3,2,1,0:T(8,128)(2,1)S(1)} custom-call(bf16[2,16,128,128]{3,2,1,0:T(8,128)(2,1)S(1)} %copy-done, s32[64,4]{1,0:T(8,128)S(1)} %copy.13.nb, s32[64]{0:T(128)S(1)} %copy-done.3, s32[64]{0:T(128)S(1)} %copy-done.4, f32[1,128]{1,0:T(1,128)S(1)} %bitcast.10, f32[1,128]{1,0:T(1,128)S(1)} %bitcast.11, ...), custom_call_target="tpu_custom_call" | custom-call | tf_op jit(solution)/shard_map/pallas_call | solution.py:399
  41.4 1.0 %copy.15 = bf16[2,16,128,128]{3,2,1,0:T(8,128)(2,1)} copy(bf16[2,16,128,128]{3,2,1,0:T(8,128)(2,1)S(1)} %shard_map.118) | data formatting | bytes 2097152
  (3 shorter events, 0.0 us)
Async XLA Ops:
  0.0 0.7 %copy-start.11 = (s32[64,4]{0,1:T(4,128)S(1)}, s32[64,4]{0,1:T(4,128)}, u32[]{:S(2)}) copy-start(s32[64,4]{0,1:T(4,128)} %param.13) | copy-start | bytes 3076
  0.7 0.7 %copy-start.3 = (s32[64]{0:T(128)S(1)}, s32[64]{0:T(128)}, u32[]{:S(2)}) copy-start(s32[64]{0:T(128)} %vr.1) | copy-start | bytes 772
  0.7 0.7 %copy-start.4 = (s32[64]{0:T(128)S(1)}, s32[64]{0:T(128)}, u32[]{:S(2)}) copy-start(s32[64]{0:T(128)} %ti.1) | copy-start | bytes 772
  0.7 0.7 %copy-start.5 = (f32[128]{0:T(128)S(1)}, f32[128]{0:T(128)}, u32[]{:S(2)}) copy-start(f32[128]{0:T(128)} %param.16) | copy-start | bytes 1540
  0.7 0.7 %copy-start.6 = (f32[128]{0:T(128)S(1)}, f32[128]{0:T(128)}, u32[]{:S(2)}) copy-start(f32[128]{0:T(128)} %param.17) | copy-start | bytes 1540
  0.7 0.7 %copy-start.7 = (f32[128]{0:T(128)S(1)}, f32[128]{0:T(128)}, u32[]{:S(2)}) copy-start(f32[128]{0:T(128)} %param.19) | copy-start | bytes 1540
  0.7 0.7 %copy-start.8 = (f32[128]{0:T(128)S(1)}, f32[128]{0:T(128)}, u32[]{:S(2)}) copy-start(f32[128]{0:T(128)} %param.20) | copy-start | bytes 1540
  0.7 0.7 %copy-start.9 = (f32[128]{0:T(128)S(1)}, f32[128]{0:T(128)}, u32[]{:S(2)}) copy-start(f32[128]{0:T(128)} %param.21) | copy-start | bytes 1540
  0.7 0.7 %copy-start.10 = (f32[128]{0:T(128)S(1)}, f32[128]{0:T(128)}, u32[]{:S(2)}) copy-start(f32[128]{0:T(128)} %param.23) | copy-start | bytes 1540
  1.4 1.2 %copy-start = (bf16[2,16,128,128]{3,2,1,0:T(8,128)(2,1)S(1)}, bf16[2,16,128,128]{3,2,1,0:T(8,128)(2,1)}, u32[]{:S(2)}) copy-start(bf16[2,16,128,128]{3,2,1,0:T(8,128)(2,1)} %x_hbm.1) | copy-start | bytes 3145732
  2.7 1.0 %copy-start.1 = (bf16[3,3,128,128]{3,2,1,0:T(8,128)(2,1)S(1)}, bf16[3,3,128,128]{3,2,1,0:T(8,128)(2,1)}, u32[]{:S(2)}) copy-start(bf16[3,3,128,128]{3,2,1,0:T(8,128)(2,1)} %param.18) | copy-start | bytes 884740
  3.6 1.0 %copy-start.2 = (bf16[3,3,128,128]{3,2,1,0:T(8,128)(2,1)S(1)}, bf16[3,3,128,128]{3,2,1,0:T(8,128)(2,1)}, u32[]{:S(2)}) copy-start(bf16[3,3,128,128]{3,2,1,0:T(8,128)(2,1)} %param.22) | copy-start | bytes 884740

commit v2 on v1

--- a/solution.py
+++ b/solution.py
@@ -27,11 +27,11 @@
 
 
 def kernel(
-    x_hbm, nb, vr, ti, gain1, shift1, k1, off1, gain2, shift2, k2, off2,
+    x_hbm, nb_hbm, vr_hbm, ti_hbm, gain1_hbm, shift1_hbm, k1, off1_hbm, gain2_hbm, shift2_hbm, k2, off2_hbm,
     out,
-    xe, p1, p2, cst, c1, c2s, c2, hc, sa, sb, hid, w1, w2, ec,
+    nb, vr, ti, gain1, shift1, off1, gain2, shift2, off2, xe, p1, p2, cst, c1, c2s, c2, hc, sa, sb, hid, w1, w2, ec,
     st_send, st, wgt, cnt,
-    x_sem, w_sem, p1_send, p1_recv, p2_send, p2_recv, c1_send, c1_recv, c2_send, c2_recv, st_ssem, st_rsem,
+    x_sem, s_sem, w_sem, p1_send, p1_recv, p2_send, p2_recv, c1_send, c1_recv, c2_send, c2_recv, st_ssem, st_rsem,
 ):
     me = lax.axis_index("tile")
 
@@ -45,6 +45,17 @@
 
     x_copy = pltpu.make_async_copy(x_hbm, xe.at[:, 2 : 2 + TH], x_sem)
     x_copy.start()
+    small_copies = [
+        pltpu.make_async_copy(a, b, s_sem.at[j])
+        for j, (a, b) in enumerate(
+            (
+                (nb_hbm, nb), (vr_hbm, vr), (ti_hbm, ti), (gain1_hbm, gain1), (shift1_hbm, shift1), (off1_hbm, off1),
+                (gain2_hbm, gain2), (shift2_hbm, shift2), (off2_hbm, off2),
+            )
+        )
+    ]
+    for copy in small_copies:
+        copy.start()
     w_copies = []
     for conv, (k_hbm, w) in enumerate(((k1, w1), (k2, w2))):
         for half in range(2):
@@ -67,6 +78,8 @@
     hc[...] = jnp.zeros(hc.shape, f32)
 
     x_copy.wait()
+    for copy in small_copies:
+        copy.wait()
 
     for t in range(2):
         for side in range(2):
@@ -120,7 +133,7 @@
 
     rows = [vr[2 * me + t] for t in range(2)]
     image = [ti[2 * me + t] for t in range(2)]
-    links = [[nb[2 * me + t, j] for j in range(4)] for t in range(2)]
+    links = [[nb[j, 2 * me + t] for j in range(4)] for t in range(2)]
     has = [[jnp.where(links[t][j] >= 0, 1.0, 0.0).astype(f32) for j in range(4)] for t in range(2)]
 
     def own_mask(t, r):
@@ -219,7 +232,7 @@
     def to_owner(o, _):
         d = lax.rem(me + o, N)
         for t in range(2):
-            p2[d, t] = p1[jnp.maximum(nb[2 * d + t, column], 0)]
+            p2[d, t] = p1[jnp.maximum(nb[column, 2 * d + t], 0)]
         pltpu.make_async_remote_copy(
             src_ref=p2.at[d],
             dst_ref=xe.at[:, ring_row, pl.ds(my_k, 16), :],
@@ -232,7 +245,7 @@
 
     lax.fori_loop(1, N, to_owner, 0)
     for t in range(2):
-        xe[t, ring_row, pl.ds(my_k, 16), :] = p1[jnp.maximum(links_of(nb, 2 * me + t, column), 0)]
+        xe[t, ring_row, pl.ds(my_k, 16), :] = p1[jnp.maximum(nb[column, 2 * me + t], 0)]
 
     @pl.when(lax.rem(me, 4) == 0)
     def _():
@@ -244,9 +257,9 @@
 
         def pick(d, t, j):
             if j == 0:
-                return c1[jnp.maximum(nb[2 * d + t, side], 0)]
-            other = jnp.maximum(nb[2 * d + t, across], 0)
-            return c1[jnp.maximum(nb[other, side], 0)]
+                return c1[jnp.maximum(nb[side, 2 * d + t], 0)]
+            other = jnp.maximum(nb[across, 2 * d + t], 0)
+            return c1[jnp.maximum(nb[side, other], 0)]
 
         def column_to_owner(o, _):
             d = lax.rem(me + o, N)
@@ -386,22 +399,24 @@
         pltpu.make_async_copy(cst, cst, c1_send).wait()
 
 
-def links_of(nb, tile, column):
-    return nb[tile, column]
-
-
 def shards(x, nb, vr, ti, gain1, shift1, kernel1, off1, gain2, shift2, kernel2, off2):
     vmem = pl.BlockSpec(memory_space=pltpu.VMEM)
-    smem = pl.BlockSpec(memory_space=pltpu.SMEM)
-    anywhere = pl.BlockSpec(memory_space=pl.ANY)
+    hbm = pl.BlockSpec(memory_space=pltpu.HBM)
     dma = pltpu.SemaphoreType.DMA
     row = lambda v: v.reshape(1, C)
+    pin = lambda v: pltpu.with_memory_space_constraint(v, pltpu.HBM)
     return pl.pallas_call(
         kernel,
         out_shape=jax.ShapeDtypeStruct(x.shape, x.dtype),
-        in_specs=[anywhere, smem, smem, smem, vmem, vmem, anywhere, vmem, vmem, vmem, anywhere, vmem],
+        in_specs=[hbm] * 12,
         out_specs=vmem,
         scratch_shapes=[
+            pltpu.SMEM((4, TILES), jnp.int32),
+            pltpu.SMEM((TILES,), jnp.int32),
+            pltpu.SMEM((TILES,), jnp.int32),
+        ]
+        + [pltpu.VMEM((1, C), f32)] * 6
+        + [
             pltpu.VMEM((2, TH + 4, TW, C), bf16),
             pltpu.VMEM((TILES, 16, C), bf16),
             pltpu.VMEM((N, 2, 16, C), bf16),
@@ -421,6 +436,7 @@
             pltpu.VMEM((2, N, C), f32),
             pltpu.VMEM((N, C), f32),
             dma,
+            dma((9,)),
             dma((12,)),
             dma,
             dma,
@@ -434,11 +450,16 @@
             dma((2,)),
         ],
         compiler_params=pltpu.CompilerParams(
-            collective_id=0, has_side_effects=True, vmem_limit_bytes=48 * 1024 * 1024
+            collective_id=0, has_side_effects=True, vmem_limit_bytes=40 * 1024 * 1024
         ),
     )(
-        x, nb, vr, ti, row(gain1), row(shift1), kernel1.reshape(3, 3 * C, C), row(off1),
-        row(gain2), row(shift2), kernel2.reshape(3, 3 * C, C), row(off2),
+        *(
+            pin(v)
+            for v in (
+                x, nb.T, vr, ti, row(gain1), row(shift1), kernel1.reshape(3, 3 * C, C), row(off1),
+                row(gain2), row(shift2), kernel2.reshape(3, 3 * C, C), row(off2),
+            )
+        )
     )
 
 

time: 42.6 us -> 36.7 us (0.86)
  local copies, waits for them, and re-layouts: 5.53 us -> 0.97 us
  Pallas kernels: 36.7 us -> 35.6 us
    unnamed x26 -> x1, local copies, waits for them, and re-layouts: 5.53 us -> 0.97 us
    pallas_call x1, Pallas kernels: 36.7 us -> 35.6 us  [shards(): pl.pallas_call(kernel, out_shape=jax.ShapeDtypeStruct(x.shape, x.dtype),...]
where the time goes in v2:
time: 36.7 us; the launch traced here: 36.6 us
  Pallas kernels  35.6 us (97%)
  local copies, waits for them, and re-layouts  0.97 us (3%)
    pallas_call x1, Pallas kernels, shards(): pl.pallas_call(kernel, out_shape=jax.ShapeDtypeStruct(x.shape, x.dtype),...  35.6 us
    unnamed x1, local copies, waits for them, and re-layouts  0.97 us

profile of v2, /device:TPU:1, one launch (start us, length us, event | category | flops | bytes accessed | tf_op | source)
XLA Modules:
  0.0 36.6 jit_solution(10879585150635405852)
XLA Ops:
  0.0 35.6 %shard_map.118 = bf16[2,16,128,128]{3,2,1,0:T(8,128)(2,1)S(1)} custom-call(bf16[2,16,128,128]{3,2,1,0:T(8,128)(2,1)} %x_hbm.1, s32[4,64]{1,0:T(4,128)} %bitcast.11, s32[64]{0:T(128)} %vr_hbm.1, s32[64]{0:T(128)} %ti_hbm.1, f32[1,128]{1,0:T(1,128)} %bitcast.12, f32[1,128]{1,0:T(1,128)} %bitcast.13, bf16[3,384,128]{2,1,0:T(8,128)(2,1)} %bitcast.9, ...), custom_call_target="tpu_custom_call" | custom-call | tf_op jit(solution)/shard_map/pallas_call | solution.py:408
  35.6 1.0 %copy.14 = bf16[2,16,128,128]{3,2,1,0:T(8,128)(2,1)} copy(bf16[2,16,128,128]{3,2,1,0:T(8,128)(2,1)S(1)} %shard_map.118) | data formatting | bytes 2097152
